TPU v7x, 32 devices: a whole 2x2x4 slice. The times are simulated.
32 devices in a mesh: row: 4 (over z), col: 8 (over y, x, core).
Axes of the slice: x: 2, y: 2, z: 4, core: 2. Of those that a mesh axis runs over, the one named last changes fastest.
Arguments:
- fock: bfloat16 [18432, 18432], P('row', 'col'), may hold values from -6 to 6
- intersection: bfloat16 [18432, 18432], P('row', 'col'), may hold values from -6 to 6
- tile_mask: int32 [2, 144, 144], P(None, 'row', 'col'), may hold values 0 or 1
- coefficients: bfloat16 [64, 7, 20, 128], P(('row', 'col')), may hold values from -0.5 to 0.5
- domains: int32 [64, 7], P(('row', 'col')), may hold values from 0 to 143, all different within a row; in each aligned block of 16 rows (0 to 15, 16 to 31, ...) at most 2 rows name the same one
- neighbours: int32 [64, 2], P(('row', 'col')), may hold values from 0 to 63, all different within a row
- amplitudes: float32 [64, 20, 20], P(('row', 'col')), may hold values from -0.18 to 0.18
Outputs:
- projected: float32 [64, 20, 20], P(('row', 'col'))
Inputs may be any that keep to these rules, and one draw needn't show every extreme that they name: `domains`: each pair names 7 different tiles; among the 16 pairs of one row index (an aligned block of pairs) no tile is named by more than 2 slots. `neighbours`: each pair names 2 different pairs.
All inputs are finite; a program needn't handle non-finite values. No bound on the sum of `tile_mask` on one device may be relied on, other than what follows from the above.
Results may differ from a plain program's by a relative error of at most 0.0041.
Values may be sent and summed in bfloat16 or wider, within the bound.
No kernel may reach another device: no remote copies, remote signals or barrier semaphores. Data moves between devices by JAX's collectives and lax.ppermute only.
A program may use at most 256 MiB of HBM per device.

v0:
```python
import jax
import jax.numpy as jnp
from jax import lax
from jax.sharding import PartitionSpec as P

HIGH = lax.Precision.HIGHEST


def bucket_slots(coeffs, tiles, base_pair, first_tile, tile_count, capacity):
    group_size, per_pair = tiles.shape
    slot_count = group_size * per_pair
    flat_tiles = tiles.reshape(slot_count)
    position = jnp.arange(slot_count, dtype=jnp.int32)
    pair_owner = base_pair + position // per_pair
    earlier = (flat_tiles[:, None] == flat_tiles[None, :]) & (position[None, :] < position[:, None])
    slot_rank = jnp.sum(earlier.astype(jnp.int32), axis=1)
    wanted = first_tile + jnp.arange(tile_count, dtype=jnp.int32)
    levels = jnp.arange(capacity, dtype=jnp.int32)
    matches = (flat_tiles[None, None, :] == wanted[:, None, None]) & (
        slot_rank[None, None, :] == levels[None, :, None]
    )
    present = jnp.any(matches, axis=2)
    source = jnp.sum(matches.astype(jnp.int32) * position[None, None, :], axis=2)
    flat_coeffs = coeffs.reshape((slot_count,) + coeffs.shape[2:])
    blocks = jnp.take(flat_coeffs, source, axis=0)
    blocks = jnp.where(present[:, :, None, None], blocks, jnp.zeros((), blocks.dtype))
    owners = jnp.where(present, jnp.take(pair_owner, source), -1)
    return (blocks, owners)


def shards(fock, intersection, tile_mask, coefficients, domains, neighbours, amplitudes):
    row_count = lax.axis_size("row")
    col_count = lax.axis_size("col")
    row_index = lax.axis_index("row")
    col_index = lax.axis_index("col")
    pair_dev, per_pair, pno_count, tile_size = coefficients.shape
    link_count = neighbours.shape[1]
    tile_rows = fock.shape[0] // tile_size
    tile_cols = fock.shape[1] // tile_size
    capacity = max(2, pair_dev)
    group_size = pair_dev * col_count
    width = fock.shape[1]
    group_coeffs, group_tiles, group_links = (
        lax.all_gather(coefficients, "col", axis=0, tiled=True),
        lax.all_gather(domains, "col", axis=0, tiled=True),
        lax.all_gather(neighbours, "col", axis=0, tiled=True),
    )

    def rows_of(coeffs, tiles, base_pair):
        return bucket_slots(coeffs, tiles, base_pair, row_index * tile_rows, tile_rows, capacity)

    def cols_of(coeffs, tiles, base_pair):
        return bucket_slots(coeffs, tiles, base_pair, col_index * tile_cols, tile_cols, capacity)

    all_coeffs, all_tiles, all_links = (
        lax.all_gather(group_coeffs, "row", axis=0, tiled=True),
        lax.all_gather(group_tiles, "row", axis=0, tiled=True),
        lax.all_gather(group_links, "row", axis=0, tiled=True),
    )
    grouped_coeffs = all_coeffs.reshape((row_count, group_size) + all_coeffs.shape[1:])
    grouped_tiles = all_tiles.reshape(row_count, group_size, per_pair)
    bases = jnp.arange(row_count, dtype=jnp.int32) * group_size
    row_blocks, row_owners = jax.vmap(rows_of)(grouped_coeffs, grouped_tiles, bases)
    col_blocks, col_owners = jax.vmap(cols_of)(grouped_coeffs, grouped_tiles, bases)

    def masked(matrix, flags):
        tiled = matrix.reshape(tile_rows, tile_size, tile_cols, tile_size)
        return (tiled * flags.astype(matrix.dtype)[:, None, :, None]).reshape(matrix.shape)

    operator = jnp.concatenate(
        [masked(fock, tile_mask[0]), masked(intersection, tile_mask[1])], axis=1
    )
    operator = operator.reshape(tile_rows, tile_size, 2 * width)
    link_groups = all_links.reshape(row_count, group_size, link_count)
    group_bases = jnp.arange(row_count, dtype=jnp.int32) * group_size

    def one_group(inputs):
        blocks, owners, links_here, base_pair = inputs
        parts = jnp.einsum("tmak,tkw->tmaw", blocks, operator, preferred_element_type=jnp.float32)
        members = base_pair + jnp.arange(group_size, dtype=jnp.int32)
        flat_owners = owners.reshape(-1)
        bucket_count = flat_owners.shape[0]
        flat_parts = parts.reshape(bucket_count, pno_count, 2 * width)
        hits = flat_owners[None, :] == members[:, None]
        order = jnp.cumsum(hits.astype(jnp.int32), axis=1) - 1
        spots = jnp.arange(bucket_count, dtype=jnp.int32)
        total = jnp.zeros((group_size, pno_count, 2 * width), jnp.float32)
        for slot in range(per_pair):
            pick = hits & (order == slot)
            found = jnp.any(pick, axis=1)
            where_at = jnp.sum(pick.astype(jnp.int32) * spots[None, :], axis=1)
            picked = jnp.take(flat_parts, where_at, axis=0)
            total = total + jnp.where(found[:, None, None], picked, jnp.zeros((), jnp.float32))
        left = total.astype(jnp.bfloat16)
        left = left.reshape(group_size, pno_count, 2, tile_cols, tile_size)
        chosen = (col_owners[None, None] == links_here[:, :, None, None, None]).astype(jnp.bfloat16)
        partner = jnp.einsum(
            "qngtm,gtmbk->qntbk", chosen, col_blocks, preferred_element_type=jnp.float32
        ).astype(jnp.bfloat16)
        return jnp.einsum("qamtk,qntbk->qnmab", left, partner, preferred_element_type=jnp.float32)

    terms = lax.map(one_group, (row_blocks, row_owners, link_groups, group_bases))
    flat_terms = terms.reshape(row_count * group_size, -1)
    sectioned = flat_terms.reshape(row_count, col_count, pair_dev, -1)
    sectioned = lax.psum_scatter(sectioned, "col", scatter_dimension=1, tiled=True)
    summed = lax.psum_scatter(sectioned, "row", scatter_dimension=0, tiled=True)
    summed = summed.reshape(pair_dev, link_count, 2, pno_count, pno_count)
    every_amp = lax.all_gather(amplitudes, ("row", "col"), axis=0, tiled=True)
    nearby = jnp.take(every_amp, neighbours, axis=0)
    fock_part = summed[:, :, 0]
    over_part = summed[:, :, 1]
    first = jnp.einsum("pnab,pnbc,pndc->pad", over_part, nearby, fock_part, precision=HIGH)
    second = jnp.einsum("pnab,pnbc,pndc->pad", fock_part, nearby, over_part, precision=HIGH)
    return first + second


def solution(mesh):
    placed = (
        P("row", "col"),
        P("row", "col"),
        P(None, "row", "col"),
        P(("row", "col"), None, None, None),
        P(("row", "col"), None),
        P(("row", "col"), None),
        P(("row", "col"), None, None),
    )
    return jax.shard_map(
        shards, mesh=mesh, in_specs=placed, out_specs=P(("row", "col"), None, None), check_vma=False
    )
```

profile of v0, /device:TPU:0, one launch (start us, length us, event | category | flops | bytes accessed | tf_op | source)
XLA Modules:
  0.0 966.6 jit_solution(7016973428302758956)
XLA Ops:
  7.4 11.6 %all_gather.26 = bf16[16,7,20,128]{3,1,2,0:T(8,128)(2,1)S(1)} all-gather(bf16[2,7,20,128]{3,1,2,0:T(8,128)(2,1)S(1)} %copy.127), channel_id=1, replica_groups=mesh['row'=4,'col'=8] {'col'}, dimensions={0}, use_global_device_ids=true | all-gather | bytes 645120 | tf_op jit(solution)/shard_map/all_gather | solution.py:44
  20.3 8.9 all-gather
  29.3 18.3 %all-gather.1 = s32[4,16,7]{1,2,0:T(8,128)S(1)} all-gather(s32[1,16,7]{1,2,0:T(8,128)S(1)} %copy.122), channel_id=1, replica_groups=mesh['row'=4,'col'=8] {'row'}, dimensions={0}, use_global_device_ids=true | all-gather | bytes 2240 | tf_op jit(solution)/shard_map/all_gather | solution.py:57
  60.7 28.3 %copy.138 = bf16[4608,2304]{0,1:T(8,128)(2,1)} copy(bf16[4608,2304]{1,0:T(8,128)(2,1)} %param.11) | data formatting | bytes 42467328 | tf_op args[0]
  89.0 8.1 mul.119
  97.1 23.5 %bitcast_multiply_fusion.1 = bf16[4608,2304]{0,1:T(8,128)(2,1)} fusion(bf16[4608,2304]{0,1:T(8,128)(2,1)} %copy.138, bf16[288,8,36,128]{3,2,1,0:T(8,128)(2,1)} %bitcast.129), kind=kLoop, calls=%fused_computation.84 | loop fusion | flops 10616832 | bytes 63700992 | tf_op jit(solution)/shard_map/mul | solution.py:68
  120.7 25.9 %copy.139 = bf16[4608,2304]{1,0:T(8,128)(2,1)} copy(bf16[4608,2304]{0,1:T(8,128)(2,1)} %bitcast_multiply_fusion.1) | data formatting | bytes 42467328 | tf_op jit(solution)/shard_map/mul | solution.py:68
  146.5 28.4 %copy.140 = bf16[4608,2304]{0,1:T(8,128)(2,1)} copy(bf16[4608,2304]{1,0:T(8,128)(2,1)} %param.12) | data formatting | bytes 42467328 | tf_op args[1]
  174.9 8.1 mul.122
  183.1 23.5 %bitcast_multiply_fusion = bf16[4608,2304]{0,1:T(8,128)(2,1)} fusion(bf16[4608,2304]{0,1:T(8,128)(2,1)} %copy.140, bf16[288,8,36,128]{3,2,1,0:T(8,128)(2,1)} %bitcast.130), kind=kLoop, calls=%fused_computation.83 | loop fusion | flops 10616832 | bytes 63700992 | tf_op jit(solution)/shard_map/mul | solution.py:68
  206.6 25.7 %copy.141 = bf16[4608,2304]{1,0:T(8,128)(2,1)} copy(bf16[4608,2304]{0,1:T(8,128)(2,1)} %bitcast_multiply_fusion) | data formatting | bytes 42467328 | tf_op jit(solution)/shard_map/mul | solution.py:68
  232.3 8.5 all-gather.2
  242.2 40.1 %all_gather.21 = f32[64,20,20]{2,1,0:T(8,128)S(1)} all-gather(f32[2,20,20]{2,1,0:T(8,128)S(1)} %copy.120), channel_id=1, replica_groups=mesh['row'=4,'col'=8] {'row','col'}, dimensions={0}, use_global_device_ids=true | all-gather | bytes 105600 | tf_op jit(solution)/shard_map/all_gather | solution.py:108
  283.6 23.7 %all-gather.3 = s32[4,16,2]{1,2,0:T(2,128)} all-gather(s32[1,16,2]{1,2,0:T(2,128)S(1)} %copy.168), channel_id=1, replica_groups=mesh['row'=4,'col'=8] {'row'}, dimensions={0}, use_global_device_ids=true | all-gather | bytes 640 | tf_op jit(solution)/shard_map/all_gather | solution.py:58
  308.6 28.3 %pad_maximum_fusion = bf16[36,128,4608]{2,1,0:T(8,128)(2,1)} fusion(bf16[36,128,2304]{2,1,0:T(8,128)(2,1)} %bitcast.132, bf16[36,128,2304]{2,1,0:T(8,128)(2,1)} %bitcast.131), kind=kLoop, calls=%fused_computation.82 | loop fusion | flops 84934656 | bytes 84934656 | tf_op jit(solution)/shard_map/concatenate | solution.py:70
  354.6 523.7 %while.12 = (s32[]{:T(128)}, f32[4,16,2,2,20,20]{5,4,3,2,0,1:T(8,128)}, s32[4,18,2]{0,2,1:T(2,128)}, s32[4,16,2]{1,2,0:T(2,128)}, bf16[4,18,2,20,128]{4,0,2,3,1:...) while((s32[]{:T(128)}, ...), condition=%wide.region_21.23_spmd, body=%wide.region_5.22_spmd.sunk | while | flops 1872830848 | bytes 213022640 | solution.py:102
  357.4 27.3 %fusion.72 = f32[36,2,20,4608]{3,2,1,0:T(8,128)} fusion(bf16[36,128,4608]{2,1,0:T(8,128)(2,1)} %get-tuple-element.364, bf16[4,36,2,20,128]{4,3,2,1,0:T(8,128)(2,1)} %get-tuple-element.363, s32[]{:T(128)} %get-tuple-element.345), kind=kOutput, calls=%fused_computation.12.clone.1 | convolution fusion | flops 1698693120 | bytes 69452288 | tf_op jit(solution)/shard_map/while/body/eval_jaxpr/tmak,tkw->tmaw/dot_general | solution.py:79
  384.7 9.5 gather_fusion.1
  394.4 9.5 gather_fusion.2
  403.9 9.5 gather_fusion.3
  413.7 9.5 gather_fusion.4
  423.2 7.5 gather_fusion.5
  430.7 9.6 gather_fusion
  449.5 21.3 %fusion.74 = bf16[16,20,4608]{2,1,0:T(8,128)(2,1)S(1)} fusion(f32[16,20,4608]{2,1,0:T(8,128)} %gather_fusion, f32[16,20,4608]{2,1,0:T(8,128)} %gather_fusion.1, f32[16,20,4608]{2,1,0:T(8,128)} %gather_fusion.2, f32[16,20,4608]{2,1,0:T(8,128)} %gather_fusion.3, f32[16,20,4608]{2,1,0:T(8,128)} %gather_fusion.4, f32[16,20,4608]{2,1,0:T(8,128)} %gather_fusion.5, ...), kind=kLoop, calls=%fused_computation.16.clone.1 | loop fusion | flops 30965760 | bytes 44237024 | tf_op jit(solution)/shard_map/while/body/eval_jaxpr/convert_element_type | solution.py:94
  488.6 27.2 %fusion.72 = f32[36,2,20,4608]{3,2,1,0:T(8,128)} fusion(bf16[36,128,4608]{2,1,0:T(8,128)(2,1)} %get-tuple-element.364, bf16[4,36,2,20,128]{4,3,2,1,0:T(8,128)(2,1)} %get-tuple-element.363, s32[]{:T(128)} %get-tuple-element.345), kind=kOutput, calls=%fused_computation.12.clone.1 | convolution fusion | flops 1698693120 | bytes 69452288 | tf_op jit(solution)/shard_map/while/body/eval_jaxpr/tmak,tkw->tmaw/dot_general | solution.py:79
  515.8 9.5 gather_fusion.1
  525.5 9.5 gather_fusion.2
  535.0 9.5 gather_fusion.3
  544.8 9.5 gather_fusion.4
  554.4 7.4 gather_fusion.5
  561.8 9.6 gather_fusion
  580.6 21.3 %fusion.74 = bf16[16,20,4608]{2,1,0:T(8,128)(2,1)S(1)} fusion(f32[16,20,4608]{2,1,0:T(8,128)} %gather_fusion, f32[16,20,4608]{2,1,0:T(8,128)} %gather_fusion.1, f32[16,20,4608]{2,1,0:T(8,128)} %gather_fusion.2, f32[16,20,4608]{2,1,0:T(8,128)} %gather_fusion.3, f32[16,20,4608]{2,1,0:T(8,128)} %gather_fusion.4, f32[16,20,4608]{2,1,0:T(8,128)} %gather_fusion.5, ...), kind=kLoop, calls=%fused_computation.16.clone.1 | loop fusion | flops 30965760 | bytes 44237024 | tf_op jit(solution)/shard_map/while/body/eval_jaxpr/convert_element_type | solution.py:94
  619.6 27.2 %fusion.72 = f32[36,2,20,4608]{3,2,1,0:T(8,128)} fusion(bf16[36,128,4608]{2,1,0:T(8,128)(2,1)} %get-tuple-element.364, bf16[4,36,2,20,128]{4,3,2,1,0:T(8,128)(2,1)} %get-tuple-element.363, s32[]{:T(128)} %get-tuple-element.345), kind=kOutput, calls=%fused_computation.12.clone.1 | convolution fusion | flops 1698693120 | bytes 69452288 | tf_op jit(solution)/shard_map/while/body/eval_jaxpr/tmak,tkw->tmaw/dot_general | solution.py:79
  646.8 9.5 gather_fusion.1
  656.6 9.5 gather_fusion.2
  666.0 9.5 gather_fusion.3
  675.8 9.5 gather_fusion.4
  692.3 9.6 gather_fusion
  711.2 21.3 %fusion.74 = bf16[16,20,4608]{2,1,0:T(8,128)(2,1)S(1)} fusion(f32[16,20,4608]{2,1,0:T(8,128)} %gather_fusion, f32[16,20,4608]{2,1,0:T(8,128)} %gather_fusion.1, f32[16,20,4608]{2,1,0:T(8,128)} %gather_fusion.2, f32[16,20,4608]{2,1,0:T(8,128)} %gather_fusion.3, f32[16,20,4608]{2,1,0:T(8,128)} %gather_fusion.4, f32[16,20,4608]{2,1,0:T(8,128)} %gather_fusion.5, ...), kind=kLoop, calls=%fused_computation.16.clone.1 | loop fusion | flops 30965760 | bytes 44237024 | tf_op jit(solution)/shard_map/while/body/eval_jaxpr/convert_element_type | solution.py:94
  750.2 27.2 %fusion.72 = f32[36,2,20,4608]{3,2,1,0:T(8,128)} fusion(bf16[36,128,4608]{2,1,0:T(8,128)(2,1)} %get-tuple-element.364, bf16[4,36,2,20,128]{4,3,2,1,0:T(8,128)(2,1)} %get-tuple-element.363, s32[]{:T(128)} %get-tuple-element.345), kind=kOutput, calls=%fused_computation.12.clone.1 | convolution fusion | flops 1698693120 | bytes 69452288 | tf_op jit(solution)/shard_map/while/body/eval_jaxpr/tmak,tkw->tmaw/dot_general | solution.py:79
  777.5 9.5 gather_fusion.1
  787.2 9.5 gather_fusion.2
  796.7 9.5 gather_fusion.3
  806.5 9.5 gather_fusion.4
  823.2 9.6 gather_fusion
  842.0 21.3 %fusion.74 = bf16[16,20,4608]{2,1,0:T(8,128)(2,1)S(1)} fusion(f32[16,20,4608]{2,1,0:T(8,128)} %gather_fusion, f32[16,20,4608]{2,1,0:T(8,128)} %gather_fusion.1, f32[16,20,4608]{2,1,0:T(8,128)} %gather_fusion.2, f32[16,20,4608]{2,1,0:T(8,128)} %gather_fusion.3, f32[16,20,4608]{2,1,0:T(8,128)} %gather_fusion.4, f32[16,20,4608]{2,1,0:T(8,128)} %gather_fusion.5, ...), kind=kLoop, calls=%fused_computation.16.clone.1 | loop fusion | flops 30965760 | bytes 44237024 | tf_op jit(solution)/shard_map/while/body/eval_jaxpr/convert_element_type | solution.py:94
  882.7 51.6 %all-reduce.4.cloned.1.call-done = f32[4,8,2,1600]{3,0,2,1:T(4,128)} async-done(((f32[4,8,2,1600]{3,0,2,1:T(4,128)}), f32[4,8,2,1600]{3,0,2,1:T(4,128)}) %all-reduce.4.cloned.1.call-update) | async-done | bytes 409616
  935.7 19.6 %all-reduce.1 = f32[4,1,2,1600]{3,2,1,0:T(2,128)S(1)} all-reduce(f32[4,1,2,1600]{3,2,1,0:T(2,128)S(1)} %copy.145), channel_id=3, replica_groups=mesh['row'=4,'col'=8] {'row'}, use_global_device_ids=true, to_apply=%region_23.25.clone | all-reduce | flops 12800 | bytes 102400
  (253 shorter events, 170.2 us)
Async XLA Ops:
  6.5 330.5 %all-gather.6.cloned.1.call-start = ((), (), s32[]{:S(2)}) async-start(), calls=%async_computation | async-start | bytes 2867200 | tf_op jit(solution)/shard_map/all_gather | solution.py:56
  20.1 914.1 %all-reduce.4.cloned.1.call-start = ((), (), s32[]{:S(2)}) async-start(), calls=%async_computation.1 | async-start | bytes 851968
  20.2 34.4 %copy-start.5 = (s32[4]{0:T(128)}, s32[4]{0:T(128)S(1)}, u32[]{:S(2)}) copy-start(s32[4]{0:T(128)S(1)} %iota_multiply_fusion) | copy-start | bytes 52
  57.2 3.5 copy-start.3
  206.6 25.7 %copy-start.4 = (s32[2,2]{1,0:T(2,128)S(1)}, s32[2,2]{1,0:T(2,128)}, u32[]{:S(2)}) copy-start(s32[2,2]{1,0:T(2,128)} %param.16) | copy-start | bytes 52
  206.6 34.3 %copy-start.9 = (u32[32]{0:T(128)S(1)}, u32[32]{0:T(128)}, u32[]{:S(2)}) copy-start(u32[32]{0:T(128)} %constant.253) | copy-start | bytes 388
  206.6 34.9 %copy-start.8 = (u32[32]{0:T(128)S(1)}, u32[32]{0:T(128)}, u32[]{:S(2)}) copy-start(u32[32]{0:T(128)} %constant.257) | copy-start | bytes 388
  206.6 35.6 %copy-start.2 = (f32[2,20,20]{2,0,1:T(2,128)S(1)}, f32[2,20,20]{2,0,1:T(2,128)}, u32[]{:S(2)}) copy-start(f32[2,20,20]{2,0,1:T(2,128)} %param.17) | copy-start | bytes 9604
  337.0 17.6 %copy-start.6 = (s32[4]{0:T(128)S(1)}, s32[4]{0:T(128)}, u32[]{:S(2)}) copy-start(s32[4]{0:T(128)} %copy-done.5) | copy-start | bytes 52
  354.6 30.1 %copy-start = (s32[4,36,2]{2,1,0:T(8,128)}, s32[4,36,2]{2,1,0:T(8,128)S(1)}, u32[]{:S(2)}) copy-start(s32[4,36,2]{2,1,0:T(8,128)S(1)} %get-tuple-element.361) | copy-start | bytes 3460 | tf_op jit(solution)/shard_map/while
  478.3 7.5 copy-start.1
  478.3 7.5 copy-start.7
  485.8 30.1 %copy-start = (s32[4,36,2]{2,1,0:T(8,128)}, s32[4,36,2]{2,1,0:T(8,128)S(1)}, u32[]{:S(2)}) copy-start(s32[4,36,2]{2,1,0:T(8,128)S(1)} %get-tuple-element.361) | copy-start | bytes 3460 | tf_op jit(solution)/shard_map/while
  609.3 7.5 copy-start.1
  609.3 7.5 copy-start.7
  616.8 30.0 %copy-start = (s32[4,36,2]{2,1,0:T(8,128)}, s32[4,36,2]{2,1,0:T(8,128)S(1)}, u32[]{:S(2)}) copy-start(s32[4,36,2]{2,1,0:T(8,128)S(1)} %get-tuple-element.361) | copy-start | bytes 3460 | tf_op jit(solution)/shard_map/while
  739.9 7.5 copy-start.1
  739.9 7.5 copy-start.7
  747.4 30.1 %copy-start = (s32[4,36,2]{2,1,0:T(8,128)}, s32[4,36,2]{2,1,0:T(8,128)S(1)}, u32[]{:S(2)}) copy-start(s32[4,36,2]{2,1,0:T(8,128)S(1)} %get-tuple-element.361) | copy-start | bytes 3460 | tf_op jit(solution)/shard_map/while
  870.8 7.5 copy-start.1
  870.8 7.5 copy-start.7
Sparse Core Ops, SparseCore 0:
  20.3 49.9 all-gather.5
  882.1 52.0 all-reduce.3
where the time goes:
time: 971 us; the launch traced here: 967 us
  local copies, waits for them, and re-layouts  428 us (44%)
  other arithmetic  193 us (20%)
  matrix products  149 us (15%)
  blocking collectives  131 us (13%)
  waiting for transfers between devices  51.6 us (5%)
  between operations  14.1 us (1%)
    gather x28, local copies, waits for them, and re-layouts, one_group(): picked = jnp.take(flat_parts, where_at, axis=0)  247 us
    dot_general x4, matrix products, one_group(): jnp.einsum('tmak,tkw->tmaw', blocks, operator, preferred_element_type=jnp...  109 us
    convert_element_type x4, other arithmetic, one_group(): left = total.astype(jnp.bfloat16)  85.2 us
    mul x4, local copies, waits for them, and re-layouts, masked(): tiled * flags.astype(matrix.dtype)[:, None, :, None]  67.9 us
    unnamed x24, local copies, waits for them, and re-layouts  61.2 us
    unnamed x3, waiting for transfers between devices  51.6 us
    mul x2, other arithmetic, masked(): tiled * flags.astype(matrix.dtype)[:, None, :, None]  47 us
    all_gather x1, blocking collectives, shards(): every_amp = lax.all_gather(amplitudes, ('row', 'col'), axis=0, tiled=True)  40.1 us
  transfers between devices with their start and end apart: 2, of which 1 were waited for; matrix products, arithmetic and copies ran while one was open for 23% of the time, Pallas kernels for 0%

commit v1 on v0

v1 whole, which is shorter than its diff:
```python
import functools

import jax
import jax.numpy as jnp
from jax import lax
from jax.experimental import pallas as pl
from jax.experimental.pallas import tpu as pltpu
from jax.sharding import PartitionSpec as P

HIGH = lax.Precision.HIGHEST
UNROLL = 8
RING_BATCHES = 32
ROW_TILE, ROW_SLOT, ROW_COUNT, COL_TILE, COL_SLOT, COL_COUNT, LINK = 0, 8, 16, 24, 32, 40, 48


def cdiv(a, b):
    return -(-a // b)


def pack(coefficients, domains, neighbours, amplitudes):
    pair_dev, per_pair, pno, tile = coefficients.shape
    spread = cdiv(pno, per_pair)
    high = lax.reduce_precision(amplitudes, 8, 7)
    middle = lax.reduce_precision(amplitudes - high, 8, 7)
    low = amplitudes - high - middle
    terms = jnp.concatenate([high, middle, low], axis=2)
    terms = jnp.pad(terms, ((0, 0), (0, per_pair * spread - pno), (0, tile - 3 * pno)))
    terms = terms.reshape(pair_dev, per_pair, spread, tile)
    numbers = jnp.concatenate([domains, neighbours], axis=1)
    numbers = jnp.pad(numbers, ((0, 0), (0, 16 - numbers.shape[1])))
    digits = jnp.concatenate([numbers & 127, numbers >> 7], axis=1)
    digits = jnp.pad(digits, ((0, 0), (0, tile - 32))).astype(jnp.float32)
    digits = jnp.broadcast_to(digits[:, None, None, :], (pair_dev, per_pair, 1, tile))
    rows = pno + spread + 1
    filler = jnp.zeros((pair_dev, per_pair, cdiv(rows, 8) * 8 - rows, tile), jnp.float32)
    extra = jnp.concatenate([terms, filler, digits], axis=2).astype(jnp.bfloat16)
    return jnp.concatenate([coefficients, extra], axis=2).reshape(pair_dev * per_pair, -1, tile)


def xor_send(x, axis, distance):
    size = lax.axis_size(axis)
    return lax.ppermute(x, axis, [(i, i ^ distance) for i in range(size)])


def gather_all(packed, rows, cols):
    mine = jnp.concatenate([packed] + [xor_send(packed, "row", d) for d in range(1, rows)], axis=0)
    unit = mine.shape[0]
    if cols == 8:
        by_x = xor_send(mine, "col", 2)
        by_y = xor_send(mine, "col", 4)
        half = unit // 2
        by_xy_low = xor_send(by_x[:half], "col", 4)
        by_xy_high = xor_send(by_y[half:], "col", 2)
        pieces = [(0, mine), (2 * unit, by_x), (4 * unit, by_y), (6 * unit, by_xy_low), (6 * unit + half, by_xy_high)]
        return pieces + [(first + unit, xor_send(piece, "col", 1)) for first, piece in pieces]
    pieces = [(0, mine)]
    distance = 1
    while distance < cols:
        pieces = pieces + [(first + distance * unit, xor_send(piece, "col", distance)) for first, piece in pieces]
        distance *= 2
    return pieces


def decode_numbers(tile_rows):
    digits = tile_rows.astype(jnp.float32)
    return digits


def project_kernel(cfg, where_ref, mask_ref, fock_ref, over_ref, *refs):
    (firsts, rows, cols, pair_dev, per_pair, links, pno, block_rows, tile, tile_rows, tile_cols) = cfg
    pieces = refs[: len(firsts)]
    out_ref, amp_ref = refs[len(firsts) : len(firsts) + 2]
    (coef, ring, numbers, table_v, table, word_a, word_b, word_c, left, keep_left, keep_out, coef_sem, table_sem, ring_sem) = refs[
        len(firsts) + 2 :
    ]
    devices = rows * cols
    pair_count = devices * pair_dev
    row_index, col_index = where_ref[0], where_ref[1]
    copies = []
    for number, (first, piece) in enumerate(zip(firsts, pieces)):
        copy = pltpu.make_async_copy(piece, coef.at[pl.ds(first, piece.shape[0])], coef_sem.at[number])
        copy.start()
        copies.append(copy)
    out_ref[...] = jnp.zeros_like(out_ref)
    left[...] = jnp.zeros_like(left)
    keep_left[...] = jnp.zeros_like(keep_left)
    keep_out[...] = jnp.zeros_like(keep_out)
    for copy in copies:
        copy.wait()

    for pair in range(pair_count):
        last = coef[pair * per_pair, block_rows - 8 : block_rows, :].astype(jnp.float32)
        numbers[pair : pair + 1, :] = last[7:8, :]

    lane = lax.broadcasted_iota(jnp.int32, (pair_count, tile), 1)
    digits = numbers[...]
    values = digits + 128.0 * pltpu.roll(digits, tile - 16, 1)
    values = jnp.where(lane < 16, values, 0.0)
    is_slot = lane < per_pair
    down = lax.broadcasted_iota(jnp.int32, (tile, tile), 0)
    across = lax.broadcasted_iota(jnp.int32, (tile, tile), 1)
    before = (down < across).astype(jnp.bfloat16)

    def put(values_here, to_lane):
        move = (across == to_lane) & (down < per_pair)
        return jnp.dot(values_here.astype(jnp.bfloat16), move.astype(jnp.bfloat16), preferred_element_type=jnp.float32)

    result = jnp.where((lane >= LINK) & (lane < LINK + links), pltpu.roll(values, LINK - per_pair, 1), 0.0)
    lane_f = lane.astype(jnp.float32)
    for first, extent, at_tile, at_slot, at_count in (
        (row_index * tile_rows, tile_rows, ROW_TILE, ROW_SLOT, ROW_COUNT),
        (col_index * tile_cols, tile_cols, COL_TILE, COL_SLOT, COL_COUNT),
    ):
        local = values - first.astype(jnp.float32)
        valid = is_slot & (local >= 0.0) & (local < float(extent))
        ones = jnp.where(valid, 1.0, 0.0)
        rank = jnp.dot(ones.astype(jnp.bfloat16), before, preferred_element_type=jnp.float32)
        result = result + put(ones, at_count)
        for place in range(per_pair):
            chosen = valid & (rank == float(place))
            result = result + put(jnp.where(chosen, local, 0.0), at_tile + place)
            result = result + put(jnp.where(chosen, lane_f, 0.0), at_slot + place)
    table_v[...] = result.astype(jnp.int32)
    copy = pltpu.make_async_copy(table_v, table, table_sem)
    copy.start()
    copy.wait()

    def fetch(number):
        word = word_a[number]
        upper, lower, column = word & 255, (word >> 8) & 255, (word >> 16) & 255
        slot = lax.rem(number, UNROLL * RING_BATCHES)
        sem = ring_sem.at[slot // UNROLL]
        for half, at in enumerate((upper, lower)):
            for which, matrix in enumerate((fock_ref, over_ref)):
                pltpu.make_async_copy(
                    matrix.at[pl.ds(pl.multiple_of(at * tile, tile), tile), pl.ds(pl.multiple_of(column * tile, tile), tile)],
                    ring.at[slot, half * tile : (half + 1) * tile, which * tile : (which + 1) * tile],
                    sem,
                ).start()

    def add_item(number, a, b, c):
        word_a[number] = a
        word_b[number] = b
        word_c[number] = c

        @pl.when(number < UNROLL * RING_BATCHES)
        def _():
            fetch(number)

    plane = tile_rows * tile_cols

    def one_link(q, carry):
        count, previous = carry
        pair, link = lax.div(q, links), lax.rem(q, links)
        place = lax.div(pair, pair_dev)
        source = (lax.rem(place, rows) ^ row_index) * cols + (lax.div(place, rows) ^ col_index)
        partner = table[pair, LINK + link]
        partner_dev = lax.div(partner, pair_dev)
        partner_place = (lax.rem(partner_dev, cols) ^ col_index) * rows + (lax.div(partner_dev, cols) ^ row_index)
        partner = partner_place * pair_dev + lax.rem(partner, pair_dev)
        row_n = table[pair, ROW_COUNT]
        col_n = table[partner, COL_COUNT]
        chunks = (row_n + 1) >> 1
        lanes = lax.rem(q, pair_dev * links) * pno

        def one_column(u, carry):
            column = table[partner, COL_TILE + u]
            partner_slot = partner * per_pair + table[partner, COL_SLOT + u]
            word_c_here = partner_slot | (lanes << 12) | (source << 20)

            def one_chunk(ch, carry):
                count, previous = carry
                two = jnp.where(2 * ch + 1 < row_n, 1, 0)
                upper = table[pair, ROW_TILE + 2 * ch]
                lower = jnp.where(two == 1, table[pair, ROW_TILE + 2 * ch + 1], upper)
                slot_a = table[pair, ROW_SLOT + 2 * ch]
                slot_b = jnp.where(two == 1, table[pair, ROW_SLOT + 2 * ch + 1], slot_a)
                at_a, at_b = upper * tile_cols + column, lower * tile_cols + column
                flags = (
                    mask_ref[at_a]
                    | (mask_ref[plane + at_a] << 1)
                    | (mask_ref[at_b] << 2)
                    | (mask_ref[plane + at_b] << 3)
                    | (two << 4)
                    | (jnp.where(ch == 0, 1, 0) << 5)
                    | (jnp.where(ch == chunks - 1, 1, 0) << 6)
                )
                fresh = jnp.where(source != previous, 1, 0)
                a = upper | (lower << 8) | (column << 16) | (flags << 24)
                b = (pair * per_pair + slot_a) | ((pair * per_pair + slot_b) << 12) | (fresh << 24)
                add_item(count, a, b, word_c_here)
                return (count + 1, source)

            return lax.fori_loop(0, chunks, one_chunk, carry)

        return lax.fori_loop(0, jnp.where(row_n > 0, col_n, 0), one_column, (count, previous))

    count, last_source = lax.fori_loop(0, pair_count * links, one_link, (jnp.int32(0), jnp.int32(-1)))
    batches = lax.div(count + UNROLL - 1, UNROLL)

    def pad_item(number, carry):
        add_item(number, jnp.int32(1 << 29), jnp.int32(0), jnp.maximum(last_source, 0) << 20)
        return carry

    lax.fori_loop(count, batches * UNROLL, pad_item, 0)

    def first_stage(t):
        base = t * UNROLL
        at = lax.rem(t, RING_BATCHES)
        window = ring.at[pl.ds(at * UNROLL, UNROLL)]
        pltpu.make_async_copy(window, window, ring_sem.at[at]).wait()
        products = []
        for i in range(UNROLL):
            a, b = word_a[base + i], word_b[base + i]
            quads = []
            for half in range(2):
                line = []
                for which in range(2):
                    keep = ((a >> (24 + 2 * half + which)) & 1) == 1
                    block = ring[at * UNROLL + i, half * tile : (half + 1) * tile, which * tile : (which + 1) * tile]
                    line.append(jnp.where(keep, block, jnp.zeros_like(block)))
                quads.append(jnp.concatenate(line, axis=1))
            weights = jnp.concatenate(quads, axis=0)
            upper = coef[b & 4095]
            lower = coef[(b >> 12) & 4095]
            lower = jnp.where(((a >> 28) & 1) == 1, lower, jnp.zeros_like(lower))
            products.append(
                jnp.dot(jnp.concatenate([upper, lower], axis=1), weights, preferred_element_type=jnp.float32)
            )
        running = keep_left[...]
        side = lax.rem(t, 2)
        for i in range(UNROLL):
            a = word_a[base + i]
            running = jnp.where(((a >> 29) & 1) == 1, products[i], running + products[i])
            done = jnp.where(((a >> 30) & 1) == 1, running, jnp.zeros_like(running)).astype(jnp.bfloat16)
            left[side, i, 0:block_rows, :] = done[:, :tile]
            left[side, i, 32 : 32 + block_rows, :] = done[:, tile:]
        keep_left[...] = running

    def second_stage(t):
        base = t * UNROLL
        side = lax.rem(t, 2)
        lanes_here = lax.broadcasted_iota(jnp.int32, (64, tile), 1)
        running = keep_out[...]
        results = []
        for i in range(UNROLL):
            c = word_c[base + i]
            partner = coef[c & 4095]
            result = lax.dot_general(
                left[side, i], partner, (((1,), (1,)), ((), ())), preferred_element_type=jnp.float32
            )
            result = jnp.concatenate([result, jnp.zeros((64, tile - block_rows), jnp.float32)], axis=1)
            result = jnp.where(lanes_here < pno, result, 0.0)
            results.append(pltpu.roll(result, (c >> 12) & 127, 1))
        for i in range(UNROLL):
            b, c = word_b[base + i], word_c[base + i]
            running = jnp.where(((b >> 24) & 1) == 1, results[i], running + results[i])
            both = jnp.concatenate([running[0:block_rows], running[32 : 32 + block_rows]], axis=0)
            out_ref[c >> 20] = both.astype(out_ref.dtype)
        keep_out[...] = running

    def step(t, carry):
        @pl.when(t < batches)
        def _():
            first_stage(t)

            @pl.when(t + RING_BATCHES < batches)
            def _():
                def again(i, carry):
                    fetch((t + RING_BATCHES) * UNROLL + i)
                    return carry

                lax.fori_loop(0, UNROLL, again, 0)

        @pl.when(t > 0)
        def _():
            second_stage(t - 1)

        return carry

    lax.fori_loop(0, jnp.where(batches > 0, batches + 1, 0), step, 0)

    for q in range(pair_dev * links):
        partner = table[q // links, LINK + q % links]
        partner_dev = lax.div(partner, pair_dev)
        partner_place = (lax.rem(partner_dev, cols) ^ col_index) * rows + (lax.div(partner_dev, cols) ^ row_index)
        partner = partner_place * pair_dev + lax.rem(partner, pair_dev)
        for s in range(per_pair):
            amp_ref[q, s] = coef[partner * per_pair + s, 16:block_rows, :].astype(jnp.float32)


def finish_kernel(cfg, got_ref, amp_ref, out_ref):
    (pair_dev, per_pair, links, pno, block_rows, tile) = cfg
    total = jnp.sum(got_ref[...].astype(jnp.float32), axis=0)
    spread = cdiv(pno, per_pair)
    skip = pno - 16
    for pair in range(pair_dev):
        answer = jnp.zeros((pno, pno), jnp.float32)
        for link in range(links):
            q = pair * links + link
            lines = jnp.concatenate([amp_ref[q, s, skip : skip + spread, :] for s in range(per_pair)], axis=0)
            lines = (lines + pltpu.roll(lines, tile - pno, 1)) + pltpu.roll(lines, tile - 2 * pno, 1)
            amps = lines[:pno, :pno]
            moved = total if q == 0 else pltpu.roll(total, tile - q * pno, 1)
            fock_part = moved[0:pno, :pno]
            over_part = moved[block_rows : block_rows + pno, :pno]
            for one, other in ((over_part, fock_part), (fock_part, over_part)):
                inner = jnp.dot(one, amps, precision=HIGH, preferred_element_type=jnp.float32)
                answer = answer + lax.dot_general(
                    inner, other, (((1,), (1,)), ((), ())), precision=HIGH, preferred_element_type=jnp.float32
                )
        out_ref[pair] = answer


def shards(fock, intersection, tile_mask, coefficients, domains, neighbours, amplitudes):
    rows, cols = lax.axis_size("row"), lax.axis_size("col")
    devices = rows * cols
    pair_dev, per_pair, pno, tile = coefficients.shape
    links = neighbours.shape[1]
    tile_rows, tile_cols = fock.shape[0] // tile, fock.shape[1] // tile
    packed = pack(coefficients, domains, neighbours, amplitudes)
    block_rows = packed.shape[1]
    pieces = gather_all(packed, rows, cols)
    firsts = tuple(first for first, _ in pieces)
    place = jnp.stack([lax.axis_index("row"), lax.axis_index("col")]).astype(jnp.int32)
    pair_count = devices * pair_dev
    slots = pair_count * per_pair
    most = pair_count * links * per_pair * cdiv(per_pair, 2) + UNROLL
    cfg = (firsts, rows, cols, pair_dev, per_pair, links, pno, block_rows, tile, tile_rows, tile_cols)
    smem = pl.BlockSpec(memory_space=pltpu.SMEM)
    anywhere = pl.BlockSpec(memory_space=pl.ANY)
    vmem = pl.BlockSpec(memory_space=pltpu.VMEM)
    parts, amp_rows = pl.pallas_call(
        functools.partial(project_kernel, cfg),
        out_shape=(
            jax.ShapeDtypeStruct((devices, 2 * block_rows, tile), jnp.bfloat16),
            jax.ShapeDtypeStruct((pair_dev * links, per_pair, block_rows - 16, tile), jnp.float32),
        ),
        in_specs=[smem, smem, anywhere, anywhere] + [anywhere] * len(pieces),
        out_specs=(vmem, vmem),
        scratch_shapes=[
            pltpu.VMEM((slots, block_rows, tile), jnp.bfloat16),
            pltpu.VMEM((UNROLL * RING_BATCHES, 2 * tile, 2 * tile), jnp.bfloat16),
            pltpu.VMEM((pair_count, tile), jnp.float32),
            pltpu.VMEM((pair_count, tile), jnp.int32),
            pltpu.SMEM((pair_count, tile), jnp.int32),
            pltpu.SMEM((most,), jnp.int32),
            pltpu.SMEM((most,), jnp.int32),
            pltpu.SMEM((most,), jnp.int32),
            pltpu.VMEM((2, UNROLL, 64, tile), jnp.bfloat16),
            pltpu.VMEM((block_rows, 2 * tile), jnp.float32),
            pltpu.VMEM((64, tile), jnp.float32),
            pltpu.SemaphoreType.DMA((len(pieces),)),
            pltpu.SemaphoreType.DMA,
            pltpu.SemaphoreType.DMA((RING_BATCHES,)),
        ],
        compiler_params=pltpu.CompilerParams(vmem_limit_bytes=60 * 1024 * 1024),
    )(place, tile_mask.reshape(-1), fock, intersection, *[piece for _, piece in pieces])
    got = lax.all_to_all(parts, ("row", "col"), 0, 0, tiled=True)
    return pl.pallas_call(
        functools.partial(finish_kernel, (pair_dev, per_pair, links, pno, block_rows, tile)),
        out_shape=jax.ShapeDtypeStruct((pair_dev, pno, pno), jnp.float32),
        in_specs=[vmem, vmem],
        out_specs=vmem,
    )(got, amp_rows)


def solution(mesh):
    placed = (
        P("row", "col"),
        P("row", "col"),
        P(None, "row", "col"),
        P(("row", "col"), None, None, None),
        P(("row", "col"), None),
        P(("row", "col"), None),
        P(("row", "col"), None, None),
    )
    return jax.shard_map(
        shards, mesh=mesh, in_specs=placed, out_specs=P(("row", "col"), None, None), check_vma=False
    )
```

time: 971 us -> 85.8 us (0.09)
  local copies, waits for them, and re-layouts: 428 us -> 4.56 us
  other arithmetic: 193 us -> 3.43 us
  matrix products: 149 us -> 0 us
  blocking collectives: 131 us -> 21.3 us
  waiting for transfers between devices: 51.6 us -> 16.1 us
  Pallas kernels: 0 us -> 27 us
  between operations: 14.1 us -> 0.16 us
  starting transfers between devices: 0.04 us -> 12.6 us
    gather x42 -> x0, local copies, waits for them, and re-layouts: 263 us -> none  [the longest x28 247 us: one_group(): picked = jnp.take(flat_parts, where_at, axis=0)]
    dot_general x16 -> x0, matrix products: 149 us -> none  [the longest x4 109 us: one_group(): jnp.einsum('tmak,tkw->tmaw', blocks, operator, preferred_element_type=jnp...]
    all_gather x6 -> x0, blocking collectives: 111 us -> none  [the longest x1 40.1 us: shards(): every_amp = lax.all_gather(amplitudes, ('row', 'col'), axis=0, tiled=True)]
    convert_element_type x8 -> x0, other arithmetic: 85.5 us -> none  [the longest x4 85.2 us: one_group(): left = total.astype(jnp.bfloat16)]
    mul x4 -> x0, local copies, waits for them, and re-layouts: 67.9 us -> none  [masked(): tiled * flags.astype(matrix.dtype)[:, None, :, None]]
    unnamed x24 -> x21, local copies, waits for them, and re-layouts: 61.2 us -> 2.41 us
    unnamed x3 -> x0, waiting for transfers between devices: 51.6 us -> none
    mul x3 -> x0, other arithmetic: 47 us -> none  [the longest x2 47 us: masked(): tiled * flags.astype(matrix.dtype)[:, None, :, None]]
  transfers between devices with their start and end apart: 2 -> 12, of which waited for: 1 -> 5; matrix products, arithmetic and copies ran while one was open for 23% -> 3% of each run, Pallas kernels for 0% -> 0%
where the time goes in v1:
time: 85.8 us; the launch traced here: 85.1 us
  Pallas kernels  27 us (31%)
  blocking collectives  21.3 us (25%)
  waiting for transfers between devices  16.1 us (19%)
  starting transfers between devices  12.6 us (15%)
  local copies, waits for them, and re-layouts  4.56 us (5%)
  other arithmetic  3.43 us (4%)
    pallas_call x1, Pallas kernels, shards(): pl.pallas_call(functools.partial(project_kernel, cfg), out_shape=(jax.Sha...  24.4 us
    all_to_all x1, blocking collectives, shards(): got = lax.all_to_all(parts, ('row', 'col'), 0, 0, tiled=True)  21.3 us
    ppermute x12, waiting for transfers between devices, xor_send(): return lax.ppermute(x, axis, [(i, i ^ distance) for i in range(size)])  16.1 us
    ppermute x12, starting transfers between devices, xor_send(): return lax.ppermute(x, axis, [(i, i ^ distance) for i in range(size)])  12.6 us
    pallas_call x1, Pallas kernels, shards(): pl.pallas_call(functools.partial(finish_kernel, (pair_dev, per_pair, link...  2.55 us
    unnamed x21, local copies, waits for them, and re-layouts  2.41 us
  transfers between devices with their start and end apart: 12, of which 5 were waited for; matrix products, arithmetic and copies ran while one was open for 3% of the time, Pallas kernels for 0%

profile of v1, /device:TPU:0, one launch (start us, length us, event | category | flops | bytes accessed | tf_op | source)
XLA Modules:
  0.0 85.1 jit_solution(4076566009634140876)
XLA Ops:
  0.0 0.8 pad_add_fusion
  0.8 0.1 pad_add_fusion.1
  0.9 0.8 reduce-precision_convert_fusion.1
  1.6 0.1 fusion.8
  1.7 1.0 %pad_maximum_fusion.1 = bf16[2,7,24,128]{3,0,2,1:T(2,128)(2,1)S(1)} fusion(bf16[2,7,1,128]{3,0,2,1:T(2,128)(2,1)S(1)} %broadcast_in_dim.2, bf16[2,7,3,128]{3,0,2,1:T(2,128)(2,1)S(1)} %bitcast.8, bf16[2,7,20,128]{3,0,2,1:T(2,128)(2,1)} %param.10), kind=kLoop, calls=%fused_computation.1 | loop fusion | flops 86016 | bytes 172032 | tf_op jit(solution)/shard_map/concatenate | solution.py:37
  2.8 5.1 %collective-permute-start.2 = (bf16[14,24,128]{2,1,0:T(8,128)(2,1)S(1)}, bf16[14,24,128]{2,1,0:T(8,128)(2,1)S(1)}, u32[]{:S(2)}, u32[]{:S(2)}) collective-permute-start(bf16[14,24,128]{2,1,0:T(8,128)(2,1)S(1)} %bitcast.4), channel_id=1, source_target_pairs={{0,24},{8,16},{16,8},{24,0},{1,25},{9,17},{17,9},{25,1},{2,26},{10... | collective-permute-start | bytes 258056 | tf_op jit(solution)/shard_map/ppermute | solution.py:42
  7.9 0.0 collective-permute-start.1
  7.9 0.6 collective-permute-start
  8.6 2.5 %collective-permute-done.2 = bf16[14,24,128]{2,1,0:T(8,128)(2,1)S(1)} collective-permute-done((bf16[14,24,128]{2,1,0:T(8,128)(2,1)S(1)}, bf16[14,24,128]{2,1,0:T(8,128)(2,1)S(1)}, u32[]{:S(2)}, u32[]{:S(2)}) %collective-permute-start.2) | collective-permute-done | bytes 86048 | tf_op jit(solution)/shard_map/ppermute | solution.py:42
  11.1 4.1 %collective-permute-done.1 = bf16[14,24,128]{2,1,0:T(8,128)(2,1)S(1)} collective-permute-done((bf16[14,24,128]{2,1,0:T(8,128)(2,1)S(1)}, bf16[14,24,128]{2,1,0:T(8,128)(2,1)S(1)}, u32[]{:S(2)}, u32[]{:S(2)}) %collective-permute-start.1) | collective-permute-done | bytes 86048 | tf_op jit(solution)/shard_map/ppermute | solution.py:42
  15.1 0.0 collective-permute-done
  15.2 0.0 copy-start
  15.2 1.6 %collective-permute-start.4 = (bf16[56,24,128]{2,1,0:T(8,128)(2,1)S(1)}, bf16[56,24,128]{2,1,0:T(8,128)(2,1)S(1)}, u32[]{:S(2)}, u32[]{:S(2)}) collective-permute-start(bf16[56,24,128]{2,1,0:T(8,128)(2,1)S(1)} %pad_maximum_fusion.refs_0_), channel_id=1, source_target_pairs={{0,4},{1,5},{2,6},{3,7},{4,0},{5,1},{6,2},{7,3},{8,12},{9,13},{10,... | collective-permute-start | bytes 1032200 | tf_op jit(solution)/shard_map/ppermute | solution.py:42
  16.8 1.5 %collective-permute-start.3 = (bf16[56,24,128]{2,1,0:T(8,128)(2,1)S(1)}, bf16[56,24,128]{2,1,0:T(8,128)(2,1)S(1)}, u32[]{:S(2)}, u32[]{:S(2)}) collective-permute-start(bf16[56,24,128]{2,1,0:T(8,128)(2,1)S(1)} %pad_maximum_fusion.refs_0_), channel_id=1, source_target_pairs={{0,2},{1,3},{2,0},{3,1},{4,6},{5,7},{6,4},{7,5},{8,10},{9,11},{10,... | collective-permute-start | bytes 1032200 | tf_op jit(solution)/shard_map/ppermute | solution.py:42
  18.3 0.0 collective-permute-start.7
  18.3 6.2 %collective-permute-done.4.refs_2_ = bf16[56,24,128]{2,1,0:T(8,128)(2,1)S(1)} collective-permute-done((bf16[56,24,128]{2,1,0:T(8,128)(2,1)S(1)}, bf16[56,24,128]{2,1,0:T(8,128)(2,1)S(1)}, u32[]{:S(2)}, u32[]{:S(2)}) %collective-permute-start.4) | collective-permute-done | bytes 344096 | tf_op jit(solution)/shard_map/ppermute | solution.py:42
  24.5 1.6 %collective-permute-start.6 = (bf16[28,24,128]{2,1,0:T(8,128)(2,1)S(1)}, bf16[28,24,128]{2,1,0:T(8,128)(2,1)S(1)}, u32[]{:S(2)}, u32[]{:S(2)}) collective-permute-start(bf16[28,24,128]{2,1,0:T(8,128)(2,1)S(1)} %slice.9), channel_id=1, source_target_pairs={{0,2},{1,3},{2,0},{3,1},{4,6},{5,7},{6,4},{7,5},{8,10},{9,11},{10,... | collective-permute-start | bytes 516104 | tf_op jit(solution)/shard_map/ppermute | solution.py:42
  26.1 0.0 collective-permute-done.3.refs_1_
  26.1 1.6 %collective-permute-start.5 = (bf16[28,24,128]{2,1,0:T(8,128)(2,1)S(1)}, bf16[28,24,128]{2,1,0:T(8,128)(2,1)S(1)}, u32[]{:S(2)}, u32[]{:S(2)}) collective-permute-start(bf16[28,24,128]{2,1,0:T(8,128)(2,1)S(1)} %slice.8), channel_id=1, source_target_pairs={{0,4},{1,5},{2,6},{3,7},{4,0},{5,1},{6,2},{7,3},{8,12},{9,13},{10,... | collective-permute-start | bytes 516104 | tf_op jit(solution)/shard_map/ppermute | solution.py:42
  27.7 0.0 collective-permute-start.9
  27.7 0.5 collective-permute-start.8
  28.2 1.7 %collective-permute-done.6.refs_4_ = bf16[28,24,128]{2,1,0:T(8,128)(2,1)S(1)} collective-permute-done((bf16[28,24,128]{2,1,0:T(8,128)(2,1)S(1)}, bf16[28,24,128]{2,1,0:T(8,128)(2,1)S(1)}, u32[]{:S(2)}, u32[]{:S(2)}) %collective-permute-start.6) | collective-permute-done | bytes 172064 | tf_op jit(solution)/shard_map/ppermute | solution.py:42
  29.9 0.0 collective-permute-start.11
  29.9 1.6 %collective-permute-done.5.refs_3_ = bf16[28,24,128]{2,1,0:T(8,128)(2,1)S(1)} collective-permute-done((bf16[28,24,128]{2,1,0:T(8,128)(2,1)S(1)}, bf16[28,24,128]{2,1,0:T(8,128)(2,1)S(1)}, u32[]{:S(2)}, u32[]{:S(2)}) %collective-permute-start.5) | collective-permute-done | bytes 172064 | tf_op jit(solution)/shard_map/ppermute | solution.py:42
  31.6 0.0 collective-permute-start.10
  31.6 0.8 copy.10
  32.4 0.7 reshape.13.mask_ref
  33.1 0.7 pad_add_fusion.2.where_ref
  33.8 0.0 collective-permute-done.7.refs_5_
  33.8 0.0 collective-permute-done.11.refs_9_
  33.8 0.0 copy-start.8
  33.8 0.0 collective-permute-done.9.refs_7_
  33.8 0.0 collective-permute-done.10.refs_8_
  33.9 0.0 collective-permute-done.8.refs_6_
  33.9 0.0 copy-done
  33.9 0.0 copy-done.1
  33.9 0.0 copy-done.2
  33.9 0.0 copy-done.6
  33.9 0.0 copy-done.7
  33.9 0.6 copy-done.3
  34.5 0.1 copy-done.8
  34.6 0.1 copy-done.4
  34.7 0.1 copy-done.9
  34.8 0.7 copy-done.5
  35.5 24.4 %shard_map.73 = (bf16[32,48,128]{2,1,0:T(8,128)(2,1)}, f32[4,7,8,128]{3,2,1,0:T(8,128)}) custom-call(s32[2]{0:T(128)} %pad_add_fusion.2.where_ref, s32[1296]{0:T(1024)} %reshape.13.mask_ref, bf16[4608,2304]{1,0:T(8,128)(2,1)} %fock_ref.1, bf16[4608,2304]{1,0:T(8,128)(2,1)} %over_ref.1, bf16[56,24,128]{2,1,0:T(8,128)(2,1)} %copy-done, ...), custom_call_target="tpu_custom_call" | custom-call | tf_op jit(solution)/shard_map/pallas_call | solution.py:333
  59.9 21.3 %all_to_all.5.got_ref = bf16[32,48,128]{2,1,0:T(8,128)(2,1)} all-to-all(bf16[32,48,128]{2,1,0:T(8,128)(2,1)} %get-tuple-element.7), channel_id=1, replica_groups=mesh['row'=4,'col'=8] {'row','col'}, dimensions={0} | all-to-all | bytes 786432 | tf_op jit(solution)/shard_map/all_to_all | solution.py:359
  81.2 2.5 %shard_map.74 = f32[2,20,20]{2,1,0:T(8,128)} custom-call(bf16[32,48,128]{2,1,0:T(8,128)(2,1)} %all_to_all.5.got_ref, f32[4,7,8,128]{3,2,1,0:T(8,128)} %get-tuple-element.8.amp_ref), custom_call_target="tpu_custom_call" | custom-call | tf_op jit(solution)/shard_map/pallas_call | solution.py:360
  83.7 1.4 %copy.12 = f32[2,20,20]{2,0,1:T(2,128)} copy(f32[2,20,20]{2,1,0:T(8,128)} %shard_map.74) | data formatting | bytes 6400 | tf_op jit(solution)/shard_map/pallas_call | solution.py:360
  (15 shorter events, 0.1 us)
Async XLA Ops:
  2.8 8.3 %collective-permute-start.2 = (bf16[14,24,128]{2,1,0:T(8,128)(2,1)S(1)}, bf16[14,24,128]{2,1,0:T(8,128)(2,1)S(1)}, u32[]{:S(2)}, u32[]{:S(2)}) collective-permute-start(bf16[14,24,128]{2,1,0:T(8,128)(2,1)S(1)} %bitcast.4), channel_id=1, source_target_pairs={{0,24},{8,16},{16,8},{24,0},{1,25},{9,17},{17,9},{25,1},{2,26},{10... | collective-permute-start | bytes 258056 | tf_op jit(solution)/shard_map/ppermute | solution.py:42
  7.9 7.2 %collective-permute-start.1 = (bf16[14,24,128]{2,1,0:T(8,128)(2,1)S(1)}, bf16[14,24,128]{2,1,0:T(8,128)(2,1)S(1)}, u32[]{:S(2)}, u32[]{:S(2)}) collective-permute-start(bf16[14,24,128]{2,1,0:T(8,128)(2,1)S(1)} %bitcast.5), channel_id=1, source_target_pairs={{0,16},{8,24},{16,0},{24,8},{1,17},{9,25},{17,1},{25,9},{2,18},{10... | collective-permute-start | bytes 258056 | tf_op jit(solution)/shard_map/ppermute | solution.py:42
  7.9 7.2 %collective-permute-start = (bf16[14,24,128]{2,1,0:T(8,128)(2,1)S(1)}, bf16[14,24,128]{2,1,0:T(8,128)(2,1)S(1)}, u32[]{:S(2)}, u32[]{:S(2)}) collective-permute-start(bf16[14,24,128]{2,1,0:T(8,128)(2,1)S(1)} %bitcast.6), channel_id=1, source_target_pairs={{0,8},{8,0},{16,24},{24,16},{1,9},{9,1},{17,25},{25,17},{2,10},{10... | collective-permute-start | bytes 258056 | tf_op jit(solution)/shard_map/ppermute | solution.py:42
  15.2 18.7 %copy-start = (bf16[56,24,128]{2,1,0:T(8,128)(2,1)}, bf16[56,24,128]{2,1,0:T(8,128)(2,1)S(1)}, u32[]{:S(2)}) copy-start(bf16[56,24,128]{2,1,0:T(8,128)(2,1)S(1)} %pad_maximum_fusion.refs_0_) | copy-start | bytes 1032196
  15.2 9.2 %collective-permute-start.4 = (bf16[56,24,128]{2,1,0:T(8,128)(2,1)S(1)}, bf16[56,24,128]{2,1,0:T(8,128)(2,1)S(1)}, u32[]{:S(2)}, u32[]{:S(2)}) collective-permute-start(bf16[56,24,128]{2,1,0:T(8,128)(2,1)S(1)} %pad_maximum_fusion.refs_0_), channel_id=1, source_target_pairs={{0,4},{1,5},{2,6},{3,7},{4,0},{5,1},{6,2},{7,3},{8,12},{9,13},{10,... | collective-permute-start | bytes 1032200 | tf_op jit(solution)/shard_map/ppermute | solution.py:42
  16.8 9.3 %collective-permute-start.3 = (bf16[56,24,128]{2,1,0:T(8,128)(2,1)S(1)}, bf16[56,24,128]{2,1,0:T(8,128)(2,1)S(1)}, u32[]{:S(2)}, u32[]{:S(2)}) collective-permute-start(bf16[56,24,128]{2,1,0:T(8,128)(2,1)S(1)} %pad_maximum_fusion.refs_0_), channel_id=1, source_target_pairs={{0,2},{1,3},{2,0},{3,1},{4,6},{5,7},{6,4},{7,5},{8,10},{9,11},{10,... | collective-permute-start | bytes 1032200 | tf_op jit(solution)/shard_map/ppermute | solution.py:42
  18.3 15.5 %collective-permute-start.7 = (bf16[56,24,128]{2,1,0:T(8,128)(2,1)S(1)}, bf16[56,24,128]{2,1,0:T(8,128)(2,1)S(1)}, u32[]{:S(2)}, u32[]{:S(2)}) collective-permute-start(bf16[56,24,128]{2,1,0:T(8,128)(2,1)S(1)} %pad_maximum_fusion.refs_0_), channel_id=1, source_target_pairs={{0,1},{1,0},{2,3},{3,2},{4,5},{5,4},{6,7},{7,6},{8,9},{9,8},{10,11... | collective-permute-start | bytes 1032200 | tf_op jit(solution)/shard_map/ppermute | solution.py:42
  24.4 9.4 %copy-start.1 = (bf16[56,24,128]{2,1,0:T(8,128)(2,1)}, bf16[56,24,128]{2,1,0:T(8,128)(2,1)S(1)}, u32[]{:S(2)}) copy-start(bf16[56,24,128]{2,1,0:T(8,128)(2,1)S(1)} %collective-permute-done.4.refs_2_) | copy-start | bytes 1032196
  24.5 5.5 %collective-permute-start.6 = (bf16[28,24,128]{2,1,0:T(8,128)(2,1)S(1)}, bf16[28,24,128]{2,1,0:T(8,128)(2,1)S(1)}, u32[]{:S(2)}, u32[]{:S(2)}) collective-permute-start(bf16[28,24,128]{2,1,0:T(8,128)(2,1)S(1)} %slice.9), channel_id=1, source_target_pairs={{0,2},{1,3},{2,0},{3,1},{4,6},{5,7},{6,4},{7,5},{8,10},{9,11},{10,... | collective-permute-start | bytes 516104 | tf_op jit(solution)/shard_map/ppermute | solution.py:42
  26.1 7.8 %copy-start.2 = (bf16[56,24,128]{2,1,0:T(8,128)(2,1)}, bf16[56,24,128]{2,1,0:T(8,128)(2,1)S(1)}, u32[]{:S(2)}) copy-start(bf16[56,24,128]{2,1,0:T(8,128)(2,1)S(1)} %collective-permute-done.3.refs_1_) | copy-start | bytes 1032196
  26.1 5.5 %collective-permute-start.5 = (bf16[28,24,128]{2,1,0:T(8,128)(2,1)S(1)}, bf16[28,24,128]{2,1,0:T(8,128)(2,1)S(1)}, u32[]{:S(2)}, u32[]{:S(2)}) collective-permute-start(bf16[28,24,128]{2,1,0:T(8,128)(2,1)S(1)} %slice.8), channel_id=1, source_target_pairs={{0,4},{1,5},{2,6},{3,7},{4,0},{5,1},{6,2},{7,3},{8,12},{9,13},{10,... | collective-permute-start | bytes 516104 | tf_op jit(solution)/shard_map/ppermute | solution.py:42
  27.7 6.1 %collective-permute-start.9 = (bf16[56,24,128]{2,1,0:T(8,128)(2,1)S(1)}, bf16[56,24,128]{2,1,0:T(8,128)(2,1)S(1)}, u32[]{:S(2)}, u32[]{:S(2)}) collective-permute-start(bf16[56,24,128]{2,1,0:T(8,128)(2,1)S(1)} %collective-permute-done.4.refs_2_), channel_id=1, source_target_pairs={{0,1},{1,0},{2,3},{3,2},{4,5},{5,4},{6,7},{7,6},{8,9},{9,8},{10,11... | collective-permute-start | bytes 1032200 | tf_op jit(solution)/shard_map/ppermute | solution.py:42
  27.7 6.2 %collective-permute-start.8 = (bf16[56,24,128]{2,1,0:T(8,128)(2,1)S(1)}, bf16[56,24,128]{2,1,0:T(8,128)(2,1)S(1)}, u32[]{:S(2)}, u32[]{:S(2)}) collective-permute-start(bf16[56,24,128]{2,1,0:T(8,128)(2,1)S(1)} %collective-permute-done.3.refs_1_), channel_id=1, source_target_pairs={{0,1},{1,0},{2,3},{3,2},{4,5},{5,4},{6,7},{7,6},{8,9},{9,8},{10,11... | collective-permute-start | bytes 1032200 | tf_op jit(solution)/shard_map/ppermute | solution.py:42
  29.9 4.0 %copy-start.6 = (bf16[28,24,128]{2,1,0:T(8,128)(2,1)}, bf16[28,24,128]{2,1,0:T(8,128)(2,1)S(1)}, u32[]{:S(2)}) copy-start(bf16[28,24,128]{2,1,0:T(8,128)(2,1)S(1)} %collective-permute-done.6.refs_4_) | copy-start | bytes 516100
  29.9 3.9 %collective-permute-start.11 = (bf16[28,24,128]{2,1,0:T(8,128)(2,1)S(1)}, bf16[28,24,128]{2,1,0:T(8,128)(2,1)S(1)}, u32[]{:S(2)}, u32[]{:S(2)}) collective-permute-start(bf16[28,24,128]{2,1,0:T(8,128)(2,1)S(1)} %collective-permute-done.6.refs_4_), channel_id=1, source_target_pairs={{0,1},{1,0},{2,3},{3,2},{4,5},{5,4},{6,7},{7,6},{8,9},{9,8},{10,11... | collective-permute-start | bytes 516104 | tf_op jit(solution)/shard_map/ppermute | solution.py:42
  31.6 2.3 %copy-start.7 = (bf16[28,24,128]{2,1,0:T(8,128)(2,1)}, bf16[28,24,128]{2,1,0:T(8,128)(2,1)S(1)}, u32[]{:S(2)}) copy-start(bf16[28,24,128]{2,1,0:T(8,128)(2,1)S(1)} %collective-permute-done.5.refs_3_) | copy-start | bytes 516100
  31.6 2.3 %collective-permute-start.10 = (bf16[28,24,128]{2,1,0:T(8,128)(2,1)S(1)}, bf16[28,24,128]{2,1,0:T(8,128)(2,1)S(1)}, u32[]{:S(2)}, u32[]{:S(2)}) collective-permute-start(bf16[28,24,128]{2,1,0:T(8,128)(2,1)S(1)} %collective-permute-done.5.refs_3_), channel_id=1, source_target_pairs={{0,1},{1,0},{2,3},{3,2},{4,5},{5,4},{6,7},{7,6},{8,9},{9,8},{10,11... | collective-permute-start | bytes 516104 | tf_op jit(solution)/shard_map/ppermute | solution.py:42
  33.8 0.7 copy-start.3
  33.8 0.8 copy-start.8
  33.8 0.9 %copy-start.4 = (bf16[56,24,128]{2,1,0:T(8,128)(2,1)}, bf16[56,24,128]{2,1,0:T(8,128)(2,1)S(1)}, u32[]{:S(2)}) copy-start(bf16[56,24,128]{2,1,0:T(8,128)(2,1)S(1)} %collective-permute-done.9.refs_7_) | copy-start | bytes 1032196
  33.8 0.9 %copy-start.9 = (bf16[28,24,128]{2,1,0:T(8,128)(2,1)}, bf16[28,24,128]{2,1,0:T(8,128)(2,1)S(1)}, u32[]{:S(2)}) copy-start(bf16[28,24,128]{2,1,0:T(8,128)(2,1)S(1)} %collective-permute-done.10.refs_8_) | copy-start | bytes 516100
  34.8 0.7 copy-start.5
